TPU v7x, 32 devices: a whole 2x2x4 slice. The times are simulated.
32 devices in a mesh: dp: 8 (over y, x, core), mp: 4 (over z).
Axes of the slice: x: 2, y: 2, z: 4, core: 2. Of those that a mesh axis runs over, the one named last changes fastest.
Arguments:
- token_ids: int32 [16], replicated, may hold values from 0 to 3071
- cache_lengths: int32 [16], P('dp'), may hold values from 1 to 512
- embedding: bfloat16 [3072, 12288], P(('dp', 'mp')), may hold values from -6 to 6
- ln_gain: float32 [12288], replicated, may hold values from 0.25 to 1.75
- query_weight: bfloat16 [12288, 6144], P('dp', 'mp'), may hold values from -0.0546875 to 0.0546875
- key_cache: bfloat16 [16, 512, 6144], P('dp', None, 'mp'), may hold values from -1000 to 1000
- value_cache: bfloat16 [16, 512, 6144], P('dp', None, 'mp'), may hold values from -6 to 6
- out_weight: bfloat16 [6144, 12288], P('mp', 'dp'), may hold values from -0.078125 to 0.078125
- final_gain: float32 [12288], replicated, may hold values from 0.25 to 1.75
Outputs:
- log_probs: float32 [16, 3072], P(None, ('dp', 'mp'))
All inputs are finite; a program needn't handle non-finite values.
Results may differ from a plain program's by a relative error of at most 0.00033.
Values may be sent and summed in bfloat16 or wider, within the bound.
A program may use at most 128 MiB of HBM per device.

v0:
```python
import jax
import jax.numpy as jnp
from jax import lax
from jax.sharding import PartitionSpec as P

HD = 128


def per_device(
    token_ids,
    cache_lengths,
    embedding,
    ln_gain,
    query_weight,
    key_cache,
    value_cache,
    out_weight,
    final_gain,
):
    voc_rows = embedding.shape[0]
    model_width = embedding.shape[1]
    vocab_start = lax.axis_index(("dp", "mp")) * voc_rows
    one_hot = (token_ids[:, None] - vocab_start == jnp.arange(voc_rows)[None, :]).astype(
        jnp.bfloat16
    )
    partial_rows = jnp.dot(one_hot, embedding, preferred_element_type=jnp.float32)
    seq_here = key_cache.shape[0]
    cache_len = key_cache.shape[1]
    cols_here = out_weight.shape[1]
    dp_index = lax.axis_index("dp")
    block_sums = lax.psum_scatter(
        partial_rows.astype(jnp.bfloat16), "dp", scatter_dimension=1, tiled=True
    )
    embedded_cols = lax.psum(block_sums, "mp").astype(jnp.float32)
    first_sum, first_sq = lax.psum(
        (jnp.sum(embedded_cols, axis=-1), jnp.sum(embedded_cols * embedded_cols, axis=-1)), "dp"
    )
    first_mean = first_sum / model_width
    first_var = first_sq / model_width - first_mean * first_mean
    ln_here = lax.dynamic_slice_in_dim(ln_gain, dp_index * cols_here, cols_here, 0)
    normed_cols = (
        ln_here * (embedded_cols - first_mean[:, None]) * lax.rsqrt(first_var[:, None] + 1e-05)
    ).astype(jnp.bfloat16)
    own_rows = lax.all_to_all(normed_cols, "dp", split_axis=0, concat_axis=1, tiled=True)
    query_sum = jnp.dot(
        own_rows,
        lax.all_gather(query_weight, "dp", axis=0, tiled=True),
        preferred_element_type=jnp.float32,
    )
    queries = (query_sum * HD ** (-0.5)).astype(jnp.bfloat16)
    heads_here = queries.shape[1] // HD
    head_query = queries.reshape(seq_here, heads_here, HD)
    key_heads = key_cache.reshape(seq_here, cache_len, heads_here, HD)
    value_heads = value_cache.reshape(seq_here, cache_len, heads_here, HD)
    scores = jnp.einsum("shd,sthd->sht", head_query, key_heads, preferred_element_type=jnp.float32)
    live_mask = jnp.arange(cache_len)[None, None, :] < cache_lengths[:, None, None]
    scores = jnp.where(live_mask, scores, jnp.float32(-1e30))
    row_top = jnp.max(scores, axis=-1, keepdims=True)
    exp_terms = jnp.exp(scores - row_top)
    weights = (exp_terms / jnp.sum(exp_terms, axis=-1, keepdims=True)).astype(jnp.bfloat16)
    attended = jnp.einsum("sht,sthd->shd", weights, value_heads, preferred_element_type=jnp.float32)
    attended = attended.astype(jnp.bfloat16).reshape(seq_here, heads_here * HD)
    every_seq = lax.all_gather(attended, "dp", axis=0, tiled=True)
    mixed_out = lax.psum(jnp.dot(every_seq, out_weight, preferred_element_type=jnp.float32), "mp")
    hidden = embedded_cols + mixed_out
    row_sum, row_sq = lax.psum((jnp.sum(hidden, axis=-1), jnp.sum(hidden * hidden, axis=-1)), "dp")
    row_mean = row_sum / model_width
    row_var = row_sq / model_width - row_mean * row_mean
    gain_here = lax.dynamic_slice_in_dim(final_gain, dp_index * cols_here, cols_here, 0)
    final_normed = (
        gain_here * (hidden - row_mean[:, None]) * lax.rsqrt(row_var[:, None] + 1e-05)
    ).astype(jnp.bfloat16)
    logits = lax.dot_general(
        lax.all_gather(final_normed, "dp", axis=1, tiled=True),
        embedding,
        (((1,), (1,)), ((), ())),
        preferred_element_type=jnp.float32,
    )
    local_top = jnp.max(logits, axis=-1)
    global_top = lax.pmax(local_top, ("dp", "mp"))
    total_exp = lax.psum(jnp.sum(jnp.exp(logits - global_top[:, None]), axis=-1), ("dp", "mp"))
    return logits - global_top[:, None] - jnp.log(total_exp)[:, None]


def solution(mesh):
    return jax.shard_map(
        per_device,
        mesh=mesh,
        in_specs=(
            P(),
            P("dp"),
            P(("dp", "mp"), None),
            P(),
            P("dp", "mp"),
            P("dp", None, "mp"),
            P("dp", None, "mp"),
            P("mp", "dp"),
            P(),
        ),
        out_specs=P(None, ("dp", "mp")),
        check_vma=False,
    )
```

profile of v0, /device:TPU:0, one launch (start us, length us, event | category | flops | bytes accessed | tf_op | source)
XLA Modules:
  0.0 406.1 jit_solution(14732259672830846114)
XLA Ops:
  6.5 0.8 broadcast_subtract_fusion
  7.3 0.9 copy-done
  8.2 1.2 convolution_convert_fusion
  11.0 36.0 %reduce-scatter.2.cloned.1.call-done = bf16[16,1536]{1,0:T(8,128)(2,1)} async-done(((bf16[16,12288]{1,0:T(8,128)(2,1)}), bf16[16,1536]{1,0:T(8,128)(2,1)}) %reduce-scatter.2.cloned.1.call-update) | async-done | bytes 49168 | tf_op jit(solution)/shard_map/reduce_scatter | solution.py:31
  47.0 19.9 %psum.49 = bf16[16,1536]{1,0:T(8,128)(2,1)S(1)} all-reduce(bf16[16,1536]{1,0:T(8,128)(2,1)} %reduce-scatter.2.cloned.1.call-done), channel_id=1, replica_groups=mesh['dp'=8,'mp'=4] {'mp'}, use_global_device_ids=true, to_apply=%region_1.0 | all-reduce | flops 24576 | bytes 98304 | tf_op jit(solution)/shard_map/psum | solution.py:34
  67.1 12.8 %all-reduce.1 = (f32[16]{0:T(128)S(1)}, f32[16]{0:T(128)S(1)}) all-reduce(f32[16]{0:T(128)S(1)} %get-tuple-element.8, f32[16]{0:T(128)S(1)} %get-tuple-element.7), channel_id=1, replica_groups=mesh['dp'=8,'mp'=4] {'dp'}, use_global_device_ids=true, to_apply=%region_5.0 | all-reduce | flops 32 | bytes 256 | tf_op jit(solution)/shard_map/psum | solution.py:35
  80.6 3.3 all-to-all-start
  84.1 4.7 %copy.14 = bf16[2,512,1536]{1,2,0:T(8,128)(2,1)} copy(bf16[2,512,1536]{2,1,0:T(8,128)(2,1)} %param.14) | data formatting | bytes 6291456 | tf_op args[5]
  88.8 4.7 %copy.15 = bf16[2,512,1536]{1,2,0:T(8,128)(2,1)} copy(bf16[2,512,1536]{2,1,0:T(8,128)(2,1)} %param.15) | data formatting | bytes 6291456 | tf_op args[6]
  93.4 135.6 %all-gather.3.cloned.1.call-done = bf16[12288,1536]{1,0:T(8,128)(2,1)} async-done(((bf16[1536,1536]{1,0:T(8,128)(2,1)}), bf16[12288,1536]{1,0:T(8,128)(2,1)}) %all-gather.3.cloned.1.call-update) | async-done | bytes 37748752 | tf_op jit(solution)/shard_map/all_gather | solution.py:47
  229.1 14.3 %fusion.2 = bf16[2,1536]{1,0:T(2,128)(2,1)S(1)} fusion(bf16[2,12288]{1,0:T(2,128)(2,1)S(1)} %bitcast.29, bf16[12288,1536]{1,0:T(8,128)(2,1)} %all-gather.3.cloned.1.call-done), kind=kOutput, calls=%fused_computation.4 | convolution fusion | flops 75503616 | bytes 37804032 | tf_op jit(solution)/shard_map/dot_general | solution.py:45
  243.4 2.4 fusion.20
  246.0 2.8 fusion.12
  248.8 9.1 %all-gather = bf16[8,2,1536]{2,1,0:T(2,128)(2,1)S(1)} all-gather(bf16[1,2,1536]{2,1,0:T(2,128)(2,1)S(1)} %reshape.56), channel_id=1, replica_groups=mesh['dp'=8,'mp'=4] {'dp'}, dimensions={0}, use_global_device_ids=true | all-gather | bytes 55296 | tf_op jit(solution)/shard_map/all_gather | solution.py:63
  258.0 3.7 fusion.21
  261.7 0.8 dynamic_slice.6
  262.5 33.8 %all-reduce.4.cloned.1.call-done = f32[16,1536]{1,0:T(8,128)} async-done(((f32[16,1536]{1,0:T(8,128)}), f32[16,1536]{1,0:T(8,128)}) %all-reduce.4.cloned.1.call-update) | async-done | bytes 98320 | tf_op jit(solution)/shard_map/psum | solution.py:64
  296.3 1.0 fusion.14
  297.3 11.8 %all-reduce = (f32[16]{0:T(128)S(1)}, f32[16]{0:T(128)S(1)}) all-reduce(f32[16]{0:T(128)S(1)} %get-tuple-element.6, f32[16]{0:T(128)S(1)} %get-tuple-element.5), channel_id=1, replica_groups=mesh['dp'=8,'mp'=4] {'dp'}, use_global_device_ids=true, to_apply=%region_12.13 | all-reduce | flops 32 | bytes 256 | tf_op jit(solution)/shard_map/psum | solution.py:66
  309.2 1.0 multiply_convert_fusion
  310.1 9.5 %all_gather.11 = bf16[16,12288]{1,0:T(8,128)(2,1)S(1)} all-gather(bf16[16,1536]{1,0:T(8,128)(2,1)S(1)} %multiply_convert_fusion), channel_id=1, replica_groups=mesh['dp'=8,'mp'=4] {'dp'}, dimensions={1}, use_global_device_ids=true | all-gather | bytes 442368 | tf_op jit(solution)/shard_map/all_gather | solution.py:74
  319.7 0.8 fusion.19
  320.5 39.2 %pmax.7 = f32[16]{0:T(128)S(1)} all-reduce(f32[16]{0:T(128)S(1)} %get-tuple-element.17), channel_id=1, replica_groups=mesh['dp'=8,'mp'=4] {'dp','mp'}, use_global_device_ids=true, to_apply=%region_14.15 | all-reduce | flops 16 | bytes 128 | tf_op jit(solution)/shard_map/pmax | solution.py:80
  359.9 39.0 %psum.55 = f32[16]{0:T(128)S(1)} all-reduce(f32[16]{0:T(128)S(1)} %exponential_reduce_fusion), channel_id=1, replica_groups=mesh['dp'=8,'mp'=4] {'dp','mp'}, use_global_device_ids=true, to_apply=%region_16.17 | all-reduce | flops 16 | bytes 128 | tf_op jit(solution)/shard_map/psum | solution.py:81
  (25 shorter events, 3.7 us)
Async XLA Ops:
  6.5 1.7 copy-start
  6.5 40.5 %reduce-scatter.2.cloned.1.call-start = ((), (), s32[]{:S(2)}) async-start(), calls=%async_computation.2 | async-start | bytes 442368 | tf_op jit(solution)/shard_map/reduce_scatter | solution.py:31
  9.5 74.5 %copy-start.1 = (s32[2]{0:T(128)S(1)}, s32[2]{0:T(128)}, u32[]{:S(2)}) copy-start(s32[2]{0:T(128)} %param.10) | copy-start | bytes 28
  9.5 219.6 %all-gather.3.cloned.1.call-start = ((), (), s32[]{:S(2)}) async-start(), calls=%async_computation.3 | async-start | bytes 42467328 | tf_op jit(solution)/shard_map/all_gather | solution.py:47
  80.6 12.9 %all-to-all-start = ((bf16[8,2,1536]{2,1,0:T(2,128)(2,1)}), bf16[8,2,1536]{2,1,0:T(2,128)(2,1)S(1)}, u32[]{:S(2)}, u32[]{:S(2)}) async-start(bf16[8,2,1536]{2,1,0:T(2,128)(2,1)} %all_to_all.14), calls=%async_computation.1 | async-start | bytes 98304 | tf_op jit(solution)/shard_map/all_to_all | solution.py:44
  83.9 212.4 %all-reduce.4.cloned.1.call-start = ((), (), s32[]{:S(2)}) async-start(), calls=%async_computation.4 | async-start | bytes 196608 | tf_op jit(solution)/shard_map/psum | solution.py:64
Sparse Core Ops, SparseCore 0:
  10.4 36.5 reduce-scatter.1
  48.9 180.1 all-gather.2
  261.8 34.4 all-reduce.3
where the time goes:
time: 407 us; the launch traced here: 406 us
  waiting for transfers between devices  206 us (51%)
  blocking collectives  141 us (35%)
  matrix products  25.2 us (6%)
  between operations  13.2 us (3%)
  local copies, waits for them, and re-layouts  12.6 us (3%)
  other arithmetic  4.18 us (1%)
    all_gather x1, waiting for transfers between devices, per_device(): lax.all_gather(query_weight, 'dp', axis=0, tiled=True)  136 us
    pmax x1, blocking collectives, per_device(): global_top = lax.pmax(local_top, ('dp', 'mp'))  39.2 us
    psum x1, blocking collectives, per_device(): lax.psum(jnp.sum(jnp.exp(logits - global_top[:, None]), axis=-1), ('dp',...  39 us
    reduce_scatter x1, waiting for transfers between devices, per_device(): lax.psum_scatter(partial_rows.astype(jnp.bfloat16), 'dp', scatter_dimensi...  36 us
    psum x1, waiting for transfers between devices, per_device(): lax.psum(jnp.dot(every_seq, out_weight, preferred_element_type=jnp.float3...  33.8 us
    psum x1, blocking collectives, per_device(): embedded_cols = lax.psum(block_sums, 'mp').astype(jnp.float32)  19.9 us
    dot_general x1, matrix products, per_device(): jnp.dot(own_rows, lax.all_gather(query_weight, 'dp', axis=0, tiled=True),...  14.3 us
    psum x1, blocking collectives, per_device(): lax.psum((jnp.sum(embedded_cols, axis=-1), jnp.sum(embedded_cols * embedd...  12.8 us
  transfers between devices with their start and end apart: 4, of which 3 were waited for; matrix products, arithmetic and copies ran while one was open for 3% of the time, Pallas kernels for 0%

commit v1 on v0

--- a/solution.py
+++ b/solution.py
@@ -61,7 +61,10 @@
     attended = jnp.einsum("sht,sthd->shd", weights, value_heads, preferred_element_type=jnp.float32)
     attended = attended.astype(jnp.bfloat16).reshape(seq_here, heads_here * HD)
     every_seq = lax.all_gather(attended, "dp", axis=0, tiled=True)
-    mixed_out = lax.psum(jnp.dot(every_seq, out_weight, preferred_element_type=jnp.float32), "mp")
+    mixed_out = jnp.sum(
+        lax.all_gather(jnp.dot(every_seq, out_weight, preferred_element_type=jnp.float32), "mp"),
+        axis=0,
+    )
     hidden = embedded_cols + mixed_out
     row_sum, row_sq = lax.psum((jnp.sum(hidden, axis=-1), jnp.sum(hidden * hidden, axis=-1)), "dp")
     row_mean = row_sum / model_width

time: 407 us -> 387 us (0.951)
  waiting for transfers between devices: 206 us -> 172 us
  blocking collectives: 141 us -> 158 us
    psum x1 -> x0, waiting for transfers between devices: 33.8 us -> none  [per_device(): lax.psum(jnp.dot(every_seq, out_weight, preferred_element_type=jnp.float3...]
    all_gather x0 -> x1, blocking collectives: none -> 14.7 us  [per_device(): lax.all_gather(jnp.dot(every_seq, out_weight, preferred_element_type=jnp....]
  transfers between devices with their start and end apart: 4 -> 3, of which waited for: 3 -> 2; matrix products, arithmetic and copies ran while one was open for 3% -> 3% of each run, Pallas kernels for 0% -> 0%
where the time goes in v1:
time: 387 us; the launch traced here: 386 us
  waiting for transfers between devices  172 us (44%)
  blocking collectives  158 us (41%)
  matrix products  24.6 us (6%)
  between operations  13.5 us (3%)
  local copies, waits for them, and re-layouts  12.5 us (3%)
    all_gather x1, waiting for transfers between devices, per_device(): lax.all_gather(query_weight, 'dp', axis=0, tiled=True)  135 us
    psum x1, blocking collectives, per_device(): lax.psum(jnp.sum(jnp.exp(logits - global_top[:, None]), axis=-1), ('dp',...  41.1 us
    pmax x1, blocking collectives, per_device(): global_top = lax.pmax(local_top, ('dp', 'mp'))  39.9 us
    reduce_scatter x1, waiting for transfers between devices, per_device(): lax.psum_scatter(partial_rows.astype(jnp.bfloat16), 'dp', scatter_dimensi...  36 us
    psum x1, blocking collectives, per_device(): embedded_cols = lax.psum(block_sums, 'mp').astype(jnp.float32)  19.9 us
    all_gather x1, blocking collectives, per_device(): lax.all_gather(jnp.dot(every_seq, out_weight, preferred_element_type=jnp....  14.7 us
    dot_general x1, matrix products, per_device(): jnp.dot(own_rows, lax.all_gather(query_weight, 'dp', axis=0, tiled=True),...  14.3 us
    psum x1, blocking collectives, per_device(): lax.psum((jnp.sum(embedded_cols, axis=-1), jnp.sum(embedded_cols * embedd...  12.8 us
  transfers between devices with their start and end apart: 3, of which 2 were waited for; matrix products, arithmetic and copies ran while one was open for 3% of the time, Pallas kernels for 0%

profile of v1, /device:TPU:0, one launch (start us, length us, event | category | flops | bytes accessed | tf_op | source)
XLA Modules:
  0.0 386.0 jit_solution(8414278317100146004)
XLA Ops:
  6.5 0.8 broadcast_subtract_fusion
  7.3 0.9 copy-done
  8.2 1.2 convolution_convert_fusion
  9.5 0.7 all-gather.4.cloned.1.call-update
  10.2 0.8 dynamic_slice.7
  11.0 36.0 %reduce-scatter.2.cloned.1.call-done = bf16[16,1536]{1,0:T(8,128)(2,1)} async-done(((bf16[16,12288]{1,0:T(8,128)(2,1)}), bf16[16,1536]{1,0:T(8,128)(2,1)}) %reduce-scatter.2.cloned.1.call-update) | async-done | bytes 49168 | tf_op jit(solution)/shard_map/reduce_scatter | solution.py:31
  47.0 19.9 %psum.42 = bf16[16,1536]{1,0:T(8,128)(2,1)S(1)} all-reduce(bf16[16,1536]{1,0:T(8,128)(2,1)} %reduce-scatter.2.cloned.1.call-done), channel_id=1, replica_groups=mesh['dp'=8,'mp'=4] {'mp'}, use_global_device_ids=true, to_apply=%region_1.0 | all-reduce | flops 24576 | bytes 98304 | tf_op jit(solution)/shard_map/psum | solution.py:34
  67.1 12.8 %all-reduce.1 = (f32[16]{0:T(128)S(1)}, f32[16]{0:T(128)S(1)}) all-reduce(f32[16]{0:T(128)S(1)} %get-tuple-element.8, f32[16]{0:T(128)S(1)} %get-tuple-element.7), channel_id=1, replica_groups=mesh['dp'=8,'mp'=4] {'dp'}, use_global_device_ids=true, to_apply=%region_5.0 | all-reduce | flops 32 | bytes 256 | tf_op jit(solution)/shard_map/psum | solution.py:35
  80.6 3.3 all-to-all-start
  84.0 4.7 %copy.14 = bf16[2,512,1536]{1,2,0:T(8,128)(2,1)} copy(bf16[2,512,1536]{2,1,0:T(8,128)(2,1)} %param.14) | data formatting | bytes 6291456 | tf_op args[5]
  88.7 4.7 %copy.15 = bf16[2,512,1536]{1,2,0:T(8,128)(2,1)} copy(bf16[2,512,1536]{2,1,0:T(8,128)(2,1)} %param.15) | data formatting | bytes 6291456 | tf_op args[6]
  93.4 0.8 dynamic_slice.6
  94.2 134.9 %all-gather.4.cloned.1.call-done = bf16[12288,1536]{1,0:T(8,128)(2,1)} async-done(((bf16[1536,1536]{1,0:T(8,128)(2,1)}), bf16[12288,1536]{1,0:T(8,128)(2,1)}) %all-gather.4.cloned.1.call-update) | async-done | bytes 37748752 | tf_op jit(solution)/shard_map/all_gather | solution.py:47
  229.1 14.3 %fusion.2 = bf16[2,1536]{1,0:T(2,128)(2,1)S(1)} fusion(bf16[2,12288]{1,0:T(2,128)(2,1)S(1)} %bitcast.31, bf16[12288,1536]{1,0:T(8,128)(2,1)} %all-gather.4.cloned.1.call-done), kind=kOutput, calls=%fused_computation.4 | convolution fusion | flops 75503616 | bytes 37804032 | tf_op jit(solution)/shard_map/dot_general | solution.py:45
  243.4 2.4 fusion.20
  246.0 2.8 fusion.12
  248.8 9.1 %all-gather.1 = bf16[8,2,1536]{2,1,0:T(2,128)(2,1)S(1)} all-gather(bf16[1,2,1536]{2,1,0:T(2,128)(2,1)S(1)} %reshape.57), channel_id=1, replica_groups=mesh['dp'=8,'mp'=4] {'dp'}, dimensions={0}, use_global_device_ids=true | all-gather | bytes 55296 | tf_op jit(solution)/shard_map/all_gather | solution.py:63
  258.0 3.1 fusion.21
  261.0 14.7 %all-gather = f32[64,1536]{1,0:T(8,128)S(1)} all-gather(f32[16,1536]{1,0:T(8,128)S(1)} %fusion.21), channel_id=2, replica_groups=mesh['dp'=8,'mp'=4] {'mp'}, dimensions={0}, use_global_device_ids=true | all-gather | bytes 491520 | tf_op jit(solution)/shard_map/all_gather | solution.py:65
  275.9 11.8 %all-reduce = (f32[16]{0:T(128)S(1)}, f32[16]{0:T(128)S(1)}) all-reduce(f32[16]{0:T(128)S(1)} %get-tuple-element.6, f32[16]{0:T(128)S(1)} %get-tuple-element.5), channel_id=1, replica_groups=mesh['dp'=8,'mp'=4] {'dp'}, use_global_device_ids=true, to_apply=%region_12.13 | all-reduce | flops 32 | bytes 256 | tf_op jit(solution)/shard_map/psum | solution.py:69
  287.9 8.6 %all_gather.19 = bf16[16,12288]{1,0:T(8,128)(2,1)S(1)} all-gather(bf16[16,1536]{1,0:T(8,128)(2,1)S(1)} %multiply_convert_fusion), channel_id=1, replica_groups=mesh['dp'=8,'mp'=4] {'dp'}, dimensions={1}, use_global_device_ids=true | all-gather | bytes 442368 | tf_op jit(solution)/shard_map/all_gather | solution.py:77
  296.5 0.8 fusion.19
  297.3 39.9 %pmax.7 = f32[16]{0:T(128)S(1)} all-reduce(f32[16]{0:T(128)S(1)} %get-tuple-element.17), channel_id=1, replica_groups=mesh['dp'=8,'mp'=4] {'dp','mp'}, use_global_device_ids=true, to_apply=%region_14.15 | all-reduce | flops 16 | bytes 128 | tf_op jit(solution)/shard_map/pmax | solution.py:83
  337.4 41.1 %psum.47 = f32[16]{0:T(128)S(1)} all-reduce(f32[16]{0:T(128)S(1)} %exponential_reduce_fusion), channel_id=1, replica_groups=mesh['dp'=8,'mp'=4] {'dp','mp'}, use_global_device_ids=true, to_apply=%region_16.17 | all-reduce | flops 16 | bytes 128 | tf_op jit(solution)/shard_map/psum | solution.py:84
  (24 shorter events, 2.4 us)
Async XLA Ops:
  6.5 1.7 copy-start
  6.5 40.5 %reduce-scatter.2.cloned.1.call-start = ((), (), s32[]{:S(2)}) async-start(), calls=%async_computation.2 | async-start | bytes 442368 | tf_op jit(solution)/shard_map/reduce_scatter | solution.py:31
  9.5 74.5 %copy-start.1 = (s32[2]{0:T(128)S(1)}, s32[2]{0:T(128)}, u32[]{:S(2)}) copy-start(s32[2]{0:T(128)} %param.10) | copy-start | bytes 28
  9.5 219.6 %all-gather.4.cloned.1.call-start = ((), (), s32[]{:S(2)}) async-start(), calls=%async_computation.3 | async-start | bytes 42467328 | tf_op jit(solution)/shard_map/all_gather | solution.py:47
  80.6 13.6 %all-to-all-start = ((bf16[8,2,1536]{2,1,0:T(2,128)(2,1)}), bf16[8,2,1536]{2,1,0:T(2,128)(2,1)S(1)}, u32[]{:S(2)}, u32[]{:S(2)}) async-start(bf16[8,2,1536]{2,1,0:T(2,128)(2,1)} %all_to_all.14), calls=%async_computation.1 | async-start | bytes 98304 | tf_op jit(solution)/shard_map/all_to_all | solution.py:44
Sparse Core Ops, SparseCore 0:
  10.4 36.5 reduce-scatter.1
  48.9 180.1 all-gather.3
